TPU v7x, 32 devices: a whole 2x2x4 slice. The times are simulated.
32 devices in a mesh: dp: 8 (over z, x), expert: 4 (over y, core).
Axes of the slice: x: 2, y: 2, z: 4, core: 2. Of those that a mesh axis runs over, the one named last changes fastest.
Arguments:
- tokens: bfloat16 [4096, 4096], P(('dp', 'expert')), may hold values from -6 to 6
- select: int32 [4, 128], P(None, ('dp', 'expert')), may hold values from -1 to 127, as said below
- gates: float32 [4, 128], P(None, ('dp', 'expert')), may hold values from 0.1 to 1
- w_gate: bfloat16 [4, 4096, 8192], P('expert', None, 'dp'), may hold values from -0.09375 to 0.09375
- w_up: bfloat16 [4, 4096, 8192], P('expert', None, 'dp'), may hold values from -0.09375 to 0.09375
- w_down: bfloat16 [4, 8192, 4096], P('expert', 'dp'), may hold values from -0.0625 to 0.0625
Outputs:
- mixed: bfloat16 [4096, 4096], P(('dp', 'expert'))
Inputs may be any that keep to these rules, and one draw needn't show every extreme that they name: `select`: in each block of 4 slots of a row, the live entries come first, distinct and ascending, below 128, followed by -1; every block holds at least one live entry, and every expert fills all 4 slots of some source device.
All inputs are finite; a program needn't handle non-finite values.
Results may differ from a plain program's by a relative error of at most 0.0085.
Values may be sent and summed in bfloat16 or wider, within the bound.
No kernel may reach another device: no remote copies, remote signals or barrier semaphores. Data moves between devices by JAX's collectives and lax.ppermute only.
A program may use at most 64 MiB of HBM per device.

v0:
```python
import jax
import jax.numpy as jnp
from jax import lax
from jax.sharding import PartitionSpec as P


def expert_ffn(block_rows, w_gate, w_up, w_down):
    gate_val = jnp.einsum("erd,edf->erf", block_rows, w_gate, preferred_element_type=jnp.float32)
    up_val = jnp.einsum("erd,edf->erf", block_rows, w_up, preferred_element_type=jnp.float32)
    hidden = (jax.nn.silu(gate_val) * up_val).astype(jnp.bfloat16)
    return jnp.einsum("erf,efd->erd", hidden, w_down, preferred_element_type=jnp.float32)


def per_device(tokens, select, gates, w_gate, w_up, w_down):
    experts, slot_count = select.shape
    tok_dev, width = tokens.shape
    is_live = select >= 0
    safe_idx = jnp.where(is_live, select, 0)
    sel_rows = jnp.take(tokens, safe_idx.reshape(-1), axis=0).reshape(experts, slot_count, width)
    sel_rows = jnp.where(is_live[:, :, None], sel_rows, 0)
    arrived = lax.all_to_all(sel_rows, "expert", split_axis=0, concat_axis=1, tiled=True)
    partial_value = expert_ffn(
        lax.all_gather(arrived, "dp", axis=1, tiled=True), w_gate, w_up, w_down
    )
    summed = lax.psum_scatter(partial_value, "dp", scatter_dimension=1, tiled=True)
    returned = lax.all_to_all(
        summed.astype(jnp.bfloat16), "expert", split_axis=1, concat_axis=0, tiled=True
    )
    weight_flat = jnp.where(is_live, gates, 0.0).reshape(-1)
    token_ids = jnp.arange(tok_dev, dtype=jnp.int32)
    combine = jnp.where(
        safe_idx.reshape(-1)[None, :] == token_ids[:, None], weight_flat[None, :], 0.0
    )
    mixed = jnp.dot(
        combine, returned.reshape(-1, width).astype(jnp.float32), precision=lax.Precision.HIGHEST
    )
    return mixed.astype(jnp.bfloat16)


def solution(mesh):
    return jax.shard_map(
        per_device,
        mesh=mesh,
        in_specs=(
            P(("dp", "expert"), None),
            P(None, ("dp", "expert")),
            P(None, ("dp", "expert")),
            P("expert", None, "dp"),
            P("expert", None, "dp"),
            P("expert", "dp", None),
        ),
        out_specs=P(("dp", "expert"), None),
        check_vma=False,
    )
```

profile of v0, /device:TPU:0, one launch (start us, length us, event | category | flops | bytes accessed | tf_op | source)
XLA Modules:
  0.0 161.7 jit_solution(17055922872757218782)
XLA Ops:
  6.5 0.0 copy-start
  6.5 0.0 all-gather.2.cloned.1.call-start
  6.5 0.8 broadcast_select_fusion
  7.3 0.7 compare_and_fusion
  8.0 0.1 reshape.81
  8.1 0.0 copy-done
  8.1 0.6 gather_fusion
  8.8 0.1 gather.7
  8.8 0.1 select_select_fusion
  9.0 8.7 %all_to_all.21 = bf16[4,4,4096]{2,1,0:T(4,128)(2,1)S(1)} all-to-all(bf16[4,4,4096]{2,1,0:T(4,128)(2,1)S(1)} %select_select_fusion), channel_id=1, replica_groups=mesh['dp'=8,'expert'=4] {'expert'}, dimensions={0} | all-to-all | bytes 262144 | tf_op jit(solution)/shard_map/all_to_all | solution.py:21
  17.6 0.7 all_to_all.7
  18.3 0.0 all-gather.2.cloned.1.call-update
  18.3 0.0 reduce-scatter.2.cloned.1.call-start
  18.4 40.7 %all-gather.2.cloned.1.call-done = bf16[1,128,4096]{2,1,0:T(8,128)(2,1)} async-done(((bf16[1,16,4096]{2,1,0:T(8,128)(2,1)}), bf16[1,128,4096]{2,1,0:T(8,128)(2,1)}) %all-gather.2.cloned.1.call-update) | async-done | bytes 1048592 | tf_op jit(solution)/shard_map/all_gather | solution.py:23
  59.1 0.0 copy-start.1
  59.1 5.0 %fusion.4 = f32[128,1024]{1,0:T(8,128)S(1)} fusion(bf16[1,4096,1024]{2,1,0:T(8,128)(2,1)} %param.9, bf16[1,128,4096]{2,1,0:T(8,128)(2,1)} %all-gather.2.cloned.1.call-done), kind=kOutput, calls=%fused_computation.5 | convolution fusion | flops 1073741824 | bytes 9961472 | tf_op jit(solution)/shard_map/erd,edf->erf/dot_general | solution.py:8
  64.1 0.0 copy-done.1
  64.1 9.6 %fusion.6 = f32[1,128,4096]{2,1,0:T(8,128)} fusion(bf16[1,1024,4096]{2,1,0:T(8,128)(2,1)} %param.11, bf16[1,4096,1024]{2,1,0:T(8,128)(2,1)} %param.10, bf16[1,128,4096]{2,1,0:T(8,128)(2,1)S(1)} %copy-done.1, f32[128,1024]{1,0:T(8,128)S(1)} %fusion.4), kind=kOutput, calls=%fused_computation.7 | convolution fusion | flops 2148270080 | bytes 20447232 | tf_op jit(solution)/shard_map/erf,efd->erd/dot_general | solution.py:11
  73.7 0.0 reduce-scatter.2.cloned.1.call-update
  73.7 67.3 %reduce-scatter.2.cloned.1.call-done = f32[1,16,4096]{2,1,0:T(8,128)} async-done(((f32[1,128,4096]{2,1,0:T(8,128)}), f32[1,16,4096]{2,1,0:T(8,128)}) %reduce-scatter.2.cloned.1.call-update) | async-done | bytes 262160 | tf_op jit(solution)/shard_map/reduce_scatter | solution.py:25
  141.0 1.0 convert_element_type.14
  142.0 0.2 copy.15
  142.2 0.5 broadcast.57
  142.7 1.4 reduce
  144.1 0.8 reshape.95
  144.9 3.3 %all-to-all-start.1 = ((bf16[4,2,8192]{2,1,0:T(2,128)(2,1)}), bf16[4,2,8192]{2,1,0:T(2,128)(2,1)S(1)}, u32[]{:S(2)}, u32[]{:S(2)}) async-start(bf16[4,2,8192]{2,1,0:T(2,128)(2,1)} %reshape.95), calls=%async_computation.2 | async-start | bytes 262144 | tf_op jit(solution)/shard_map/all_to_all | solution.py:26
  148.2 0.1 eq.15
  148.3 0.1 broadcast_in_dim.45
  148.4 4.4 %all-to-all-done.1 = bf16[4,2,8192]{2,1,0:T(2,128)(2,1)S(1)} async-done(((bf16[4,2,8192]{2,1,0:T(2,128)(2,1)}), bf16[4,2,8192]{2,1,0:T(2,128)(2,1)S(1)}, u32[]{:S(2)}, u32[]{:S(2)}) %all-to-all-start.1) | async-done | bytes 131104 | tf_op jit(solution)/shard_map/all_to_all | solution.py:26
  152.8 0.1 reshape.96
  152.9 2.0 %convolution_convert_fusion = bf16[128,4096]{1,0:T(8,128)(2,1)} fusion(bf16[1,16,4096]{2,0,1:T(2,128)(2,1)S(1)} %bitcast.36, f32[16]{0:T(128)S(1)} %broadcast_in_dim.45, s32[16]{0:T(128)S(1)} %eq.15), kind=kOutput, calls=%fused_computation.8 | convolution fusion | flops 101191680 | bytes 1179776 | tf_op jit(solution)/shard_map/dot_general | solution.py:34
  (2 shorter events, 0.0 us)
Async XLA Ops:
  6.5 1.6 copy-start
  6.5 52.5 %all-gather.2.cloned.1.call-start = ((), (), s32[]{:S(2)}) async-start(), calls=%async_computation.3 | async-start | bytes 1179648 | tf_op jit(solution)/shard_map/all_gather | solution.py:23
  18.3 122.7 %reduce-scatter.2.cloned.1.call-start = ((), (), s32[]{:S(2)}) async-start(), calls=%async_computation.4 | async-start | bytes 2359296 | tf_op jit(solution)/shard_map/reduce_scatter | solution.py:25
  59.1 5.0 %copy-start.1 = (bf16[1,128,4096]{2,1,0:T(8,128)(2,1)S(1)}, bf16[1,128,4096]{2,1,0:T(8,128)(2,1)}, u32[]{:S(2)}) copy-start(bf16[1,128,4096]{2,1,0:T(8,128)(2,1)} %all-gather.2.cloned.1.call-done) | copy-start | bytes 3145732
  144.9 7.9 %all-to-all-start.1 = ((bf16[4,2,8192]{2,1,0:T(2,128)(2,1)}), bf16[4,2,8192]{2,1,0:T(2,128)(2,1)S(1)}, u32[]{:S(2)}, u32[]{:S(2)}) async-start(bf16[4,2,8192]{2,1,0:T(2,128)(2,1)} %reshape.95), calls=%async_computation.2 | async-start | bytes 262144 | tf_op jit(solution)/shard_map/all_to_all | solution.py:26
Sparse Core Ops, SparseCore 0:
  18.5 40.5 all-gather.1
  73.8 67.1 reduce-scatter.1
where the time goes:
time: 162 us
  waiting for transfers between devices  112 us (69%)
  matrix products  16.6 us (10%)
  between operations  13.5 us (8%)
  blocking collectives  8.67 us (5%)
  other arithmetic  3.97 us (2%)
  starting transfers between devices  3.37 us (2%)
  local copies, waits for them, and re-layouts  3.28 us (2%)
    reduce_scatter x1, waiting for transfers between devices, per_device(): lax.psum_scatter(partial_value, 'dp', scatter_dimension=1, tiled=True)  67.3 us
    all_gather x1, waiting for transfers between devices, per_device(): lax.all_gather(arrived, 'dp', axis=1, tiled=True)  40.7 us
    dot_general x1, matrix products, expert_ffn(): jnp.einsum('erf,efd->erd', hidden, w_down, preferred_element_type=jnp.flo...  9.57 us
    all_to_all x1, blocking collectives, per_device(): lax.all_to_all(sel_rows, 'expert', split_axis=0, concat_axis=1, tiled=True)  8.67 us
    dot_general x1, matrix products, expert_ffn(): jnp.einsum('erd,edf->erf', block_rows, w_gate, preferred_element_type=jnp...  5.03 us
    all_to_all x1, waiting for transfers between devices, per_device(): lax.all_to_all(summed.astype(jnp.bfloat16), 'expert', split_axis=1, conca...  4.4 us
    all_to_all x1, starting transfers between devices, per_device(): lax.all_to_all(summed.astype(jnp.bfloat16), 'expert', split_axis=1, conca...  3.33 us
  transfers between devices with their start and end apart: 3, of which 3 were waited for; matrix products, arithmetic and copies ran while one was open for 0% of the time, Pallas kernels for 0%

commit v1 on v0

--- a/solution.py
+++ b/solution.py
@@ -18,7 +18,15 @@
     safe_idx = jnp.where(is_live, select, 0)
     sel_rows = jnp.take(tokens, safe_idx.reshape(-1), axis=0).reshape(experts, slot_count, width)
     sel_rows = jnp.where(is_live[:, :, None], sel_rows, 0)
-    arrived = lax.all_to_all(sel_rows, "expert", split_axis=0, concat_axis=1, tiled=True)
+    arrived = jnp.concatenate(
+        lax.all_to_all(
+            jnp.stack(jnp.split(sel_rows, lax.axis_size("expert"), axis=0)),
+            axis_name="expert",
+            split_axis=0,
+            concat_axis=0,
+        ),
+        axis=1,
+    )
     partial_value = expert_ffn(
         lax.all_gather(arrived, "dp", axis=1, tiled=True), w_gate, w_up, w_down
     )

time: 162 us -> 162 us (level)
  no operation moved by 1% of the time
where the time goes in v1:
time: 162 us
  waiting for transfers between devices  112 us (69%)
  matrix products  16.6 us (10%)
  between operations  13.5 us (8%)
  blocking collectives  8.67 us (5%)
  other arithmetic  4.09 us (3%)
  starting transfers between devices  3.37 us (2%)
  local copies, waits for them, and re-layouts  3.33 us (2%)
    reduce_scatter x1, waiting for transfers between devices, per_device(): lax.psum_scatter(partial_value, 'dp', scatter_dimension=1, tiled=True)  67.3 us
    all_gather x1, waiting for transfers between devices, per_device(): lax.all_gather(arrived, 'dp', axis=1, tiled=True)  40.7 us
    dot_general x1, matrix products, expert_ffn(): jnp.einsum('erf,efd->erd', hidden, w_down, preferred_element_type=jnp.flo...  9.57 us
    all_to_all x1, blocking collectives, per_device(): lax.all_to_all(jnp.stack(jnp.split(sel_rows, lax.axis_size('expert'), axi...  8.67 us
    dot_general x1, matrix products, expert_ffn(): jnp.einsum('erd,edf->erf', block_rows, w_gate, preferred_element_type=jnp...  5.04 us
    all_to_all x1, waiting for transfers between devices, per_device(): lax.all_to_all(summed.astype(jnp.bfloat16), 'expert', split_axis=1, conca...  4.4 us
    all_to_all x1, starting transfers between devices, per_device(): lax.all_to_all(summed.astype(jnp.bfloat16), 'expert', split_axis=1, conca...  3.33 us
  transfers between devices with their start and end apart: 3, of which 3 were waited for; matrix products, arithmetic and copies ran while one was open for 0% of the time, Pallas kernels for 0%

profile of v1, /device:TPU:0, one launch (start us, length us, event | category | flops | bytes accessed | tf_op | source)
XLA Modules:
  0.0 162.0 jit_solution(2293305821855917495)
XLA Ops:
  6.5 0.0 copy-start
  6.5 0.0 all-gather.2.cloned.1.call-start
  6.5 0.8 broadcast_select_fusion
  7.3 0.7 compare_and_fusion
  8.0 0.1 reshape.81
  8.1 0.0 copy-done
  8.1 0.6 gather_fusion
  8.8 0.1 gather.7
  8.8 0.1 select_select_fusion
  9.0 0.1 pad_maximum_fusion
  9.1 8.7 %all_to_all.14 = bf16[4,1,4,4096]{3,2,1,0:T(4,128)(2,1)S(1)} all-to-all(bf16[4,1,4,4096]{3,2,1,0:T(4,128)(2,1)S(1)} %pad_maximum_fusion), channel_id=1, replica_groups=mesh['dp'=8,'expert'=4] {'expert'}, dimensions={0} | all-to-all | bytes 262144 | tf_op jit(solution)/shard_map/all_to_all | solution.py:22
  17.8 0.7 reshape.82
  18.5 0.0 all-gather.2.cloned.1.call-update
  18.5 0.0 reduce-scatter.2.cloned.1.call-start
  18.6 40.7 %all-gather.2.cloned.1.call-done = bf16[1,128,4096]{2,1,0:T(8,128)(2,1)} async-done(((bf16[1,16,4096]{2,1,0:T(8,128)(2,1)}), bf16[1,128,4096]{2,1,0:T(8,128)(2,1)}) %all-gather.2.cloned.1.call-update) | async-done | bytes 1048592 | tf_op jit(solution)/shard_map/all_gather | solution.py:31
  59.2 0.0 copy-start.1
  59.2 5.0 %fusion.4 = f32[128,1024]{1,0:T(8,128)S(1)} fusion(bf16[1,4096,1024]{2,1,0:T(8,128)(2,1)} %param.9, bf16[1,128,4096]{2,1,0:T(8,128)(2,1)} %all-gather.2.cloned.1.call-done), kind=kOutput, calls=%fused_computation.5 | convolution fusion | flops 1073741824 | bytes 9961472 | tf_op jit(solution)/shard_map/erd,edf->erf/dot_general | solution.py:8
  64.3 0.0 copy-done.1
  64.3 9.6 %fusion.6 = f32[1,128,4096]{2,1,0:T(8,128)} fusion(bf16[1,1024,4096]{2,1,0:T(8,128)(2,1)} %param.11, bf16[1,4096,1024]{2,1,0:T(8,128)(2,1)} %param.10, bf16[1,128,4096]{2,1,0:T(8,128)(2,1)S(1)} %copy-done.1, f32[128,1024]{1,0:T(8,128)S(1)} %fusion.4), kind=kOutput, calls=%fused_computation.7 | convolution fusion | flops 2148270080 | bytes 20447232 | tf_op jit(solution)/shard_map/erf,efd->erd/dot_general | solution.py:11
  73.9 0.0 reduce-scatter.2.cloned.1.call-update
  73.9 67.3 %reduce-scatter.2.cloned.1.call-done = f32[1,16,4096]{2,1,0:T(8,128)} async-done(((f32[1,128,4096]{2,1,0:T(8,128)}), f32[1,16,4096]{2,1,0:T(8,128)}) %reduce-scatter.2.cloned.1.call-update) | async-done | bytes 262160 | tf_op jit(solution)/shard_map/reduce_scatter | solution.py:33
  141.2 1.0 convert_element_type.14
  142.2 0.2 copy.15
  142.5 0.5 broadcast.57
  143.0 1.4 reduce
  144.3 0.8 reshape.96
  145.1 3.3 %all-to-all-start.1 = ((bf16[4,2,8192]{2,1,0:T(2,128)(2,1)}), bf16[4,2,8192]{2,1,0:T(2,128)(2,1)S(1)}, u32[]{:S(2)}, u32[]{:S(2)}) async-start(bf16[4,2,8192]{2,1,0:T(2,128)(2,1)} %reshape.96), calls=%async_computation.2 | async-start | bytes 262144 | tf_op jit(solution)/shard_map/all_to_all | solution.py:34
  148.5 0.1 eq.15
  148.5 0.1 broadcast_in_dim.45
  148.6 4.4 %all-to-all-done.1 = bf16[4,2,8192]{2,1,0:T(2,128)(2,1)S(1)} async-done(((bf16[4,2,8192]{2,1,0:T(2,128)(2,1)}), bf16[4,2,8192]{2,1,0:T(2,128)(2,1)S(1)}, u32[]{:S(2)}, u32[]{:S(2)}) %all-to-all-start.1) | async-done | bytes 131104 | tf_op jit(solution)/shard_map/all_to_all | solution.py:34
  153.0 0.1 reshape.97
  153.1 2.0 %convolution_convert_fusion = bf16[128,4096]{1,0:T(8,128)(2,1)} fusion(bf16[1,16,4096]{2,0,1:T(2,128)(2,1)S(1)} %bitcast.44, f32[16]{0:T(128)S(1)} %broadcast_in_dim.45, s32[16]{0:T(128)S(1)} %eq.15), kind=kOutput, calls=%fused_computation.8 | convolution fusion | flops 101191680 | bytes 1179776 | tf_op jit(solution)/shard_map/dot_general | solution.py:42
  (3 shorter events, 0.1 us)
Async XLA Ops:
  6.5 1.6 copy-start
  6.5 52.7 %all-gather.2.cloned.1.call-start = ((), (), s32[]{:S(2)}) async-start(), calls=%async_computation.3 | async-start | bytes 1179648 | tf_op jit(solution)/shard_map/all_gather | solution.py:31
  18.5 122.7 %reduce-scatter.2.cloned.1.call-start = ((), (), s32[]{:S(2)}) async-start(), calls=%async_computation.4 | async-start | bytes 2359296 | tf_op jit(solution)/shard_map/reduce_scatter | solution.py:33
  59.2 5.0 %copy-start.1 = (bf16[1,128,4096]{2,1,0:T(8,128)(2,1)S(1)}, bf16[1,128,4096]{2,1,0:T(8,128)(2,1)}, u32[]{:S(2)}) copy-start(bf16[1,128,4096]{2,1,0:T(8,128)(2,1)} %all-gather.2.cloned.1.call-done) | copy-start | bytes 3145732
  145.1 7.9 %all-to-all-start.1 = ((bf16[4,2,8192]{2,1,0:T(2,128)(2,1)}), bf16[4,2,8192]{2,1,0:T(2,128)(2,1)S(1)}, u32[]{:S(2)}, u32[]{:S(2)}) async-start(bf16[4,2,8192]{2,1,0:T(2,128)(2,1)} %reshape.96), calls=%async_computation.2 | async-start | bytes 262144 | tf_op jit(solution)/shard_map/all_to_all | solution.py:34
Sparse Core Ops, SparseCore 0:
  18.6 40.5 all-gather.1
  74.0 67.1 reduce-scatter.1
